TPU v7x, 256 devices: a whole 4x4x8 slice. The times are simulated.
256 devices in a mesh: trial: 4 (over x), fsdp: 16 (over z, core), cols: 4 (over y).
Axes of the slice: x: 4, y: 4, z: 8, core: 2. Of those that a mesh axis runs over, the one named last changes fastest.
Arguments:
- train_gate: bfloat16 [8192, 8192], P(('trial', 'fsdp'), 'cols'), parts along dimension 0, may hold values from -0.1875 to 0.1875
- low_gate: bfloat16 [8192, 16], P(('trial', 'fsdp')), parts along dimension 0, may hold values from -0.125 to 0.125
- high_gate: bfloat16 [64, 8192], P('trial', 'cols'), parts along dimension 0, may hold values from -1.5 to 1.5
- train_up: bfloat16 [8192, 8192], P(('trial', 'fsdp'), 'cols'), parts along dimension 0, may hold values from -0.1875 to 0.1875
- low_up: bfloat16 [8192, 16], P(('trial', 'fsdp')), parts along dimension 0, may hold values from -0.125 to 0.125
- high_up: bfloat16 [64, 8192], P('trial', 'cols'), parts along dimension 0, may hold values from -1.5 to 1.5
- norm_gain: float32 [8192], P(('trial', 'fsdp')), parts along dimension 0, may hold values from 0.25 to 1.75
Outputs:
- ready_gate: bfloat16 [8192, 8192], P('trial', 'cols'), parts along dimension 0
- ready_up: bfloat16 [8192, 8192], P('trial', 'cols'), parts along dimension 0
- column_gate: float32 [32768], P(('trial', 'cols')), parts along dimension 0
- column_up: float32 [32768], P(('trial', 'cols')), parts along dimension 0
There are 4 independent parts, one for each index of `trial`. A program takes and returns all parts, laid end to end along the dimension named above; each array names one. Nothing has to cross between parts.
All inputs are finite; a program needn't handle non-finite values. Where the computation divides by a largest or mean magnitude, that divisor is 1e-20 or more.
Results may differ from a plain program's by a relative error of at most 0.001.
Values may be sent and summed in bfloat16 or wider, within the bound.
A program may use at most 128 MiB of HBM per device.

v0:
```python
import jax
import jax.numpy as jnp
from jax import lax
from jax.sharding import PartitionSpec as P

mix_rate = 1.0


def from_everyone(array, axis):
    copies = jnp.broadcast_to(array, (lax.axis_size(axis), *array.shape))
    return lax.all_to_all(copies, axis, split_axis=0, concat_axis=0, tiled=True)


def over_copies(array, axis):
    return from_everyone(array, axis).max(axis=0)


def in_one(arrays, axis):
    line, at, outs = (jnp.concatenate([a.reshape(-1) for a in arrays]), 0, [])
    total = over_copies(line, axis)
    for a in arrays:
        outs.append(total[at : at + a.size].reshape(a.shape))
        at += a.size
    return tuple(outs)


def sent_together(arrays, axis, dim, along):
    both = jnp.concatenate(arrays, axis=along)
    filled, at, outs = (lax.all_gather(both, axis, axis=dim, tiled=True), 0, [])
    for a in arrays:
        outs.append(lax.slice_in_dim(filled, at, at + a.shape[along], axis=along))
        at += a.shape[along]
    return tuple(outs)


def per_device(train_gate, low_gate, high_gate, train_up, low_up, high_up, norm_gain):
    latest_gate = train_gate.astype(jnp.float32) + mix_rate * jnp.dot(
        low_gate, high_gate, preferred_element_type=jnp.float32
    )
    latest_up = train_up.astype(jnp.float32) + mix_rate * jnp.dot(
        low_up, high_up, preferred_element_type=jnp.float32
    )
    latest_gained_gate = latest_gate * norm_gain[:, None]
    latest_gained_up = latest_up * norm_gain[:, None]
    column_gate, column_up = in_one(
        (jnp.max(jnp.abs(latest_gained_gate), axis=0), jnp.max(jnp.abs(latest_gained_up), axis=0)),
        "fsdp",
    )
    narrow_gate, narrow_up = (
        (latest_gained_gate / column_gate).astype(jnp.bfloat16),
        (latest_gained_up / column_up).astype(jnp.bfloat16),
    )
    ready_gate, ready_up = sent_together((narrow_gate, narrow_up), "fsdp", 0, 1)
    return (ready_gate, ready_up, column_gate, column_up)


def solution(mesh):
    placed = (
        P(("trial", "fsdp"), "cols"),
        P(("trial", "fsdp"), None),
        P("trial", "cols"),
        P(("trial", "fsdp"), "cols"),
        P(("trial", "fsdp"), None),
        P("trial", "cols"),
        P(("trial", "fsdp")),
    )
    return jax.shard_map(
        per_device,
        mesh=mesh,
        in_specs=placed,
        out_specs=(
            P("trial", "cols"),
            P("trial", "cols"),
            P(("trial", "cols")),
            P(("trial", "cols")),
        ),
        check_vma=False,
    )
```

profile of v0, /device:TPU:1, one launch (start us, length us, event | category | flops | bytes accessed | tf_op | source)
XLA Modules:
  0.0 145.5 jit_solution(3239936507184123214)
XLA Ops:
  7.2 0.0 copy-start
  7.2 0.0 all-gather.2.cloned.1.call-start
  7.2 0.8 copy-done
  8.0 1.4 abs_reduce_fusion.1
  9.4 1.4 abs_reduce_fusion
  10.9 0.2 broadcast_in_dim.2
  11.1 21.4 %all_to_all.6 = f32[16,1,4096]{2,1,0:T(1,128)S(1)} all-to-all(f32[16,1,4096]{2,1,0:T(1,128)S(1)} %broadcast_in_dim.2), channel_id=1, replica_groups=mesh['trial'=4,'fsdp'=16,'cols'=4] {'fsdp'}, dimensions={0} | all-to-all | bytes 524288 | tf_op jit(solution)/shard_map/all_to_all | solution.py:11
  32.4 0.2 reduce_max.29
  32.6 0.0 copy-start.1
  32.6 0.0 copy-start.2
  32.6 0.2 divide_convert_fusion
  32.8 1.1 pad_maximum_fusion
  33.9 0.0 all-gather.2.cloned.1.call-update
  33.9 92.7 %all-gather.2.cloned.1.call-done = bf16[2048,4096]{1,0:T(8,128)(2,1)} async-done(((bf16[128,4096]{1,0:T(8,128)(2,1)}), bf16[2048,4096]{1,0:T(8,128)(2,1)}) %all-gather.2.cloned.1.call-update) | async-done | bytes 16777232 | tf_op jit(solution)/shard_map/all_gather | solution.py:29
  126.6 11.9 %fusion.2 = (bf16[2048,2048]{1,0:T(8,128)(2,1)}, bf16[2048,2048]{1,0:T(8,128)(2,1)}) fusion(bf16[2048,4096]{1,0:T(8,128)(2,1)} %all-gather.2.cloned.1.call-done), kind=kLoop, calls=%fused_computation.10 | loop fusion | bytes 33554432 | tf_op jit(solution)/shard_map/slice | solution.py:31
  138.6 0.0 copy-done.1
  138.6 0.0 copy-done.2
  (2 shorter events, 0.0 us)
Async XLA Ops:
  7.2 0.8 copy-start
  7.2 119.5 %all-gather.2.cloned.1.call-start = ((), (), s32[]{:S(2)}) async-start(), calls=%async_computation.1 | async-start | bytes 17825792 | tf_op jit(solution)/shard_map/all_gather | solution.py:29
  32.6 106.0 %copy-start.1 = (f32[2048]{0:T(1024)}, f32[2048]{0:T(1024)S(1)}, u32[]{:S(2)}) copy-start(f32[2048]{0:T(1024)S(1)} %get-tuple-element.6) | copy-start | bytes 24580
  32.6 106.0 %copy-start.2 = (f32[2048]{0:T(1024)}, f32[2048]{0:T(1024)S(1)}, u32[]{:S(2)}) copy-start(f32[2048]{0:T(1024)S(1)} %get-tuple-element.7) | copy-start | bytes 24580
Sparse Core Ops, SparseCore 0:
  34.1 92.5 all-gather.1
where the time goes:
time: 146 us; the launch traced here: 145 us
  waiting for transfers between devices  92.7 us (63%)
  blocking collectives  21.4 us (15%)
  between operations  14.1 us (10%)
  local copies, waits for them, and re-layouts  13 us (9%)
  matrix products  2.84 us (2%)
    all_gather x1, waiting for transfers between devices, sent_together(): filled, at, outs = (lax.all_gather(both, axis, axis=dim, tiled=True), 0, [])  92.7 us
    all_to_all x1, blocking collectives, from_everyone(): return lax.all_to_all(copies, axis, split_axis=0, concat_axis=0, tiled=True)  21.4 us
    slice x1, local copies, waits for them, and re-layouts, sent_together(): outs.append(lax.slice_in_dim(filled, at, at + a.shape[along], axis=along))  11.9 us
  transfers between devices with their start and end apart: 1, of which 1 were waited for; matrix products, arithmetic and copies ran while one was open for 0% of the time, Pallas kernels for 0%

commit v1 on v0

v1 whole, which is shorter than its diff:
```python
import functools

import jax
import jax.numpy as jnp
from jax import lax
from jax.experimental import pallas as pl
from jax.experimental.pallas import tpu as pltpu
from jax.sharding import PartitionSpec as P

MESH = pl.DeviceIdType.MESH
BF16, F32 = jnp.bfloat16, jnp.float32

N = 16
ROWS = 128
COLS = 2048
RANK = 16
NCB = 8
W = COLS // NCB
GROUP = 4
SIDE = 56


def gather(
    tg, lg, hg, tu, lu, hu, gn,
    out, cmax,
    raw, side, gain, high, low, gainb, part,
    load_sem, side_sem, ring_recv, ring_send, side_send, pair_recv, pair_send, own_recv, own_send,
):
    trial, me, cols = lax.axis_index("trial"), lax.axis_index("fsdp"), lax.axis_index("cols")
    right, left = lax.rem(me + 2, N), lax.rem(me + N - 2, N)
    pair = me + 1 - 2 * lax.rem(me, 2)
    ahead = (right, left)

    def to(f):
        return (trial, f, cols)

    def source(f, way, hops):
        return lax.rem(f + N - 2 * hops, N) if way == 0 else lax.rem(f + 2 * hops, N)

    loads = []
    for p, (low_in, high_in) in enumerate(((lg, hg), (lu, hu))):
        loads.append(pltpu.make_async_copy(low_in, side.at[me, pl.ds(p * RANK, RANK)], side_sem.at[p]))
        loads.append(pltpu.make_async_copy(high_in, high.at[p], side_sem.at[2 + p]))
    loads.append(pltpu.make_async_copy(gn, gain.at[me], side_sem.at[4]))

    def own_load(p, cb):
        train = (tg, tu)[p]
        return pltpu.make_async_copy(
            train.at[:, pl.ds(pl.multiple_of(cb * W, W), W)], raw.at[p, me, cb], load_sem.at[p, cb]
        )

    for copy in loads:
        copy.start()
    for cb in range(NCB):
        for p in range(2):
            own_load(p, cb).start()

    barrier = pltpu.get_barrier_semaphore()
    for f in (right, left, pair):
        pl.semaphore_signal(barrier, inc=1, device_id=to(f), device_id_type=MESH)
    pl.semaphore_wait(barrier, 3)

    def remote(ref, send, recv, f):
        return pltpu.make_async_remote_copy(
            src_ref=ref, dst_ref=ref, send_sem=send, recv_sem=recv, device_id=to(f), device_id_type=MESH
        )

    def chunk_at(hops, cb, short):
        return (hops - 1) * 2 * NCB + cb * 2 + short

    def ring_chunk(way, p, src, cb, at):
        return remote(raw.at[p, src, cb], ring_send.at[way], ring_recv.at[way, at], ahead[way])

    def pair_chunk(way, p, src, cb, at):
        return remote(raw.at[p, src, cb], pair_send, pair_recv.at[way, at], pair)

    def own_chunk(p, src, cb):
        return remote(raw.at[p, src, cb], pair_send, own_recv.at[p * NCB + cb], pair)

    def side_ref(way, src, hops):
        return side.at[src, pl.ds(way * RANK, RANK)] if hops == 4 else side.at[src]

    def ring_side(way, src, hops):
        copies = [remote(side_ref(way, src, hops), side_send.at[way, hops - 1], ring_recv.at[way, SIDE + hops - 1], ahead[way])]
        if way == 0 or hops < 4:
            copies.append(remote(gain.at[src], side_send.at[way, 3 + hops], ring_recv.at[way, SIDE + 3 + hops], ahead[way]))
        return copies

    def pair_side(way, src, hops):
        copies = [remote(side_ref(way, src, hops), own_send.at[way, hops - 1], pair_recv.at[way, SIDE + hops - 1], pair)]
        if way == 0 or hops < 4:
            copies.append(remote(gain.at[src], own_send.at[way, 3 + hops], pair_recv.at[way, SIDE + 3 + hops], pair))
        return copies

    def own_side(src):
        return [
            remote(side.at[src], own_send.at[0, 8], own_recv.at[2 * NCB], pair),
            remote(gain.at[src], own_send.at[1, 8], own_recv.at[2 * NCB + 1], pair),
        ]

    for copy in loads:
        copy.wait()
    for way in range(2):
        for copy in ring_side(way, me, 1):
            copy.start()
    for copy in own_side(me):
        copy.start()

    def send_own(cb, _):
        for p in range(2):
            own_load(p, cb).wait()
        for k in range(2):
            for way in range(2):
                p = way if k == 0 else 1 - way
                ring_chunk(way, p, me, cb, chunk_at(1, cb, k)).start()
        for p in range(2):
            own_chunk(p, me, cb).start()
        return 0

    lax.fori_loop(0, NCB, send_own, 0)

    def rows(src, n=1):
        return pl.ds(pl.multiple_of(src * ROWS, ROWS), n * ROWS)

    def prepare(src):
        for p in range(2):
            low[p, rows(src), :] = side[src, pl.ds(p * RANK, RANK), :].astype(F32).T.astype(BF16)
        gainb[rows(src), :] = jnp.broadcast_to(gain[src], (ROWS, ROWS)).T

    def merged(p, src, cb, n):
        train = raw[p, pl.ds(src, n), cb].reshape(n * ROWS, W).astype(F32)
        delta = jnp.dot(
            low[p, rows(src, n), :],
            high[p, :, pl.ds(pl.multiple_of(cb * W, W), W)],
            preferred_element_type=F32,
        )
        scale = gainb[rows(src, n), :]
        return (train + delta) * jnp.concatenate([scale] * (W // ROWS), axis=1)

    def note(p, src, cb):
        size = jnp.abs(merged(p, src, cb, 1)).reshape(ROWS // 8, 8, W).max(axis=0)
        part[p, cb] = jnp.maximum(part[p, cb], size)

    part[...] = jnp.zeros_like(part)
    prepare(me)

    def note_own(cb, _):
        for p in range(2):
            note(p, me, cb)
        return 0

    lax.fori_loop(0, NCB, note_own, 0)

    for copy in own_side(pair):
        copy.wait_recv()
    prepare(pair)

    def note_pair(cb, _):
        for p in range(2):
            own_chunk(p, pair, cb).wait_recv()
            note(p, pair, cb)
        return 0

    lax.fori_loop(0, NCB, note_pair, 0)

    for hops in (1, 2, 3):
        for way in range(2):
            src = source(me, way, hops)
            for copy in ring_side(way, src, hops):
                copy.wait_recv()
            for copy in ring_side(way, src, hops + 1) + pair_side(way, src, hops):
                copy.start()
            prepare(src)
        for way in range(2):
            src = source(pair, way, hops)
            for copy in pair_side(way, src, hops):
                copy.wait_recv()
            prepare(src)

        def step(cb, _, hops=hops):
            for k in range(2):
                for way in range(2):
                    p, src = (way if k == 0 else 1 - way), source(me, way, hops)
                    at = chunk_at(hops, cb, k)
                    ring_chunk(way, p, src, cb, at).wait_recv()
                    if hops < 3:
                        ring_chunk(way, p, src, cb, chunk_at(hops + 1, cb, k)).start()
                    elif k == 0:
                        ring_chunk(way, p, src, cb, 6 * NCB + cb).start()
                    pair_chunk(way, p, src, cb, at).start()
            for k in range(2):
                for way in range(2):
                    note(way if k == 0 else 1 - way, source(me, way, hops), cb)
            for k in range(2):
                for way in range(2):
                    p, src = (way if k == 0 else 1 - way), source(pair, way, hops)
                    pair_chunk(way, p, src, cb, chunk_at(hops, cb, k)).wait_recv()
                    note(p, src, cb)
            return 0

        lax.fori_loop(0, NCB, step, 0)

    far, far_pair = source(me, 0, 4), source(pair, 0, 4)
    for way in range(2):
        for copy in ring_side(way, far, 4):
            copy.wait_recv()
        for copy in pair_side(way, far, 4):
            copy.start()
    prepare(far)
    for way in range(2):
        for copy in pair_side(way, far_pair, 4):
            copy.wait_recv()
    prepare(far_pair)

    def finish(cb):
        for p in range(2):
            pair_chunk(p, p, far_pair, cb, 6 * NCB + cb).wait_recv()
            note(p, far_pair, cb)
        for p in range(2):
            largest = part[p, cb].max(axis=0, keepdims=True)
            cmax[p, :, pl.ds(pl.multiple_of(cb * W, W), W)] = largest
            part[p, cb] = jnp.broadcast_to(1.0 / largest, (8, W))

        def scale(i, _):
            for p in range(2):
                whole = merged(p, i * GROUP, cb, GROUP) * part[p, cb, :1]
                out[p, rows(i * GROUP, GROUP), pl.ds(pl.multiple_of(cb * W, W), W)] = whole.astype(BF16)
            return 0

        lax.fori_loop(0, N // GROUP, scale, 0)

    def last(cb, _):
        for p in range(2):
            ring_chunk(p, p, far, cb, 6 * NCB + cb).wait_recv()
            pair_chunk(p, p, far, cb, 6 * NCB + cb).start()
        for p in range(2):
            note(p, far, cb)

        @pl.when(cb > 0)
        def _():
            finish(cb - 1)

        return 0

    lax.fori_loop(0, NCB, last, 0)
    finish(NCB - 1)

    for way in range(2):
        sent = raw.at[0, pl.ds(0, 7)]
        pltpu.make_async_copy(sent, sent, ring_send.at[way]).wait()
        for hops in (1, 2, 3, 4):
            src = source(me, way, hops - 1)
            for copy in ring_side(way, src, hops):
                copy.wait_send()
            for copy in pair_side(way, source(me, way, hops), hops):
                copy.wait_send()
    for copy in own_side(me):
        copy.wait_send()
    pltpu.make_async_copy(raw.at[0], raw.at[0], pair_send).wait()


PIECES = 8


def write(new, cmax, gate, up, col_gate, col_up, sem):
    copies = []
    for p, (dst, col) in enumerate(((gate, col_gate), (up, col_up))):
        for i in range(PIECES):
            at = pl.ds(i * (COLS // PIECES), COLS // PIECES)
            copies.append(pltpu.make_async_copy(new.at[p, at], dst.at[at], sem.at[p, i]))
        copies.append(pltpu.make_async_copy(cmax.at[p], col, sem.at[p, PIECES]))
    for copy in copies:
        copy.start()
    for copy in copies:
        copy.wait()


def per_device(train_gate, low_gate, high_gate, train_up, low_up, high_up, norm_gain):
    anywhere = pl.BlockSpec(memory_space=pl.ANY)
    vmem = pl.BlockSpec(memory_space=pltpu.VMEM)
    dma = pltpu.SemaphoreType.DMA
    new, cmax = pl.pallas_call(
        gather,
        name="gather",
        out_shape=(pltpu.VMEM((2, N * ROWS, COLS), BF16), pltpu.VMEM((2, 1, COLS), F32)),
        in_specs=[anywhere] * 7,
        out_specs=(vmem, vmem),
        scratch_shapes=[
            pltpu.VMEM((2, N, NCB, ROWS, W), BF16),
            pltpu.VMEM((N, 2 * RANK, ROWS), BF16),
            pltpu.VMEM((N, 1, ROWS), F32),
            pltpu.VMEM((2, RANK, COLS), BF16),
            pltpu.VMEM((2, N * ROWS, RANK), BF16),
            pltpu.VMEM((N * ROWS, ROWS), F32),
            pltpu.VMEM((2, NCB, 8, W), F32),
            dma((2, NCB)),
            dma((5,)),
            dma((2, SIDE + 8)),
            dma((2,)),
            dma((2, 8)),
            dma((2, SIDE + 8)),
            dma,
            dma((2 * NCB + 2,)),
            dma((2, 9)),
        ],
        compiler_params=pltpu.CompilerParams(
            collective_id=0, has_side_effects=True, vmem_limit_bytes=40 * 2**20
        ),
    )(train_gate, low_gate.T, high_gate, train_up, low_up.T, high_up, norm_gain.reshape(1, ROWS))
    hbm = pl.BlockSpec(memory_space=pltpu.HBM)
    gate, up, col_gate, col_up = pl.pallas_call(
        write,
        name="write",
        out_shape=(
            jax.ShapeDtypeStruct((N * ROWS, COLS), BF16),
            jax.ShapeDtypeStruct((N * ROWS, COLS), BF16),
            jax.ShapeDtypeStruct((1, COLS), F32),
            jax.ShapeDtypeStruct((1, COLS), F32),
        ),
        in_specs=[vmem, vmem],
        out_specs=(hbm,) * 4,
        scratch_shapes=[dma((2, PIECES + 1))],
        compiler_params=pltpu.CompilerParams(vmem_limit_bytes=20 * 2**20),
    )(new, cmax)
    return gate, up, col_gate.reshape(COLS), col_up.reshape(COLS)


def solution(mesh):
    placed = (
        P(("trial", "fsdp"), "cols"),
        P(("trial", "fsdp"), None),
        P("trial", "cols"),
        P(("trial", "fsdp"), "cols"),
        P(("trial", "fsdp"), None),
        P("trial", "cols"),
        P(("trial", "fsdp")),
    )
    return jax.shard_map(
        per_device,
        mesh=mesh,
        in_specs=placed,
        out_specs=(
            P("trial", "cols"),
            P("trial", "cols"),
            P(("trial", "cols")),
            P(("trial", "cols")),
        ),
        check_vma=False,
    )
```

time: 146 us -> 104 us (0.71)
  Pallas kernels: 0 us -> 103 us
  waiting for transfers between devices: 92.7 us -> 0 us
  blocking collectives: 21.4 us -> 0 us
  between operations: 14.1 us -> 0.64 us
  local copies, waits for them, and re-layouts: 13 us -> 0 us
  matrix products: 2.84 us -> 0 us
    pallas_call x0 -> x2, Pallas kernels: none -> 103 us  [the longest x1 97.3 us: per_device(): pl.pallas_call(gather, name='gather', out_shape=(pltpu.VMEM((2, N * ROWS,...]
    all_gather x1 -> x0, waiting for transfers between devices: 92.7 us -> none  [sent_together(): filled, at, outs = (lax.all_gather(both, axis, axis=dim, tiled=True), 0, [])]
    all_to_all x1 -> x0, blocking collectives: 21.4 us -> none  [from_everyone(): return lax.all_to_all(copies, axis, split_axis=0, concat_axis=0, tiled=True)]
    slice x2 -> x0, local copies, waits for them, and re-layouts: 12 us -> none  [the longest x1 11.9 us: sent_together(): outs.append(lax.slice_in_dim(filled, at, at + a.shape[along], axis=along))]
    dot_general x2 -> x0, matrix products: 2.84 us -> none  [the longest x1 1.44 us: per_device(): jnp.dot(low_up, high_up, preferred_element_type=jnp.float32)]
  transfers between devices with their start and end apart: 1 -> 0, of which waited for: 1 -> 0; matrix products, arithmetic and copies ran while one was open for 0% -> 0% of each run, Pallas kernels for 0% -> 0%
where the time goes in v1:
time: 104 us
  Pallas kernels  103 us (99%)
    pallas_call x1, Pallas kernels, per_device(): pl.pallas_call(gather, name='gather', out_shape=(pltpu.VMEM((2, N * ROWS,...  97.3 us
    pallas_call x1, Pallas kernels, per_device(): pl.pallas_call(write, name='write', out_shape=(jax.ShapeDtypeStruct((N *...  5.99 us

profile of v1, /device:TPU:1, one launch (start us, length us, event | category | flops | bytes accessed | tf_op | source)
XLA Modules:
  0.0 103.9 jit_solution(534875390345456068)
XLA Ops:
  0.6 97.3 %gather.1 = (bf16[2,2048,2048]{2,1,0:T(8,128)(2,1)S(1)}, f32[2,1,2048]{2,1,0:T(1,128)S(1)}) custom-call(bf16[128,2048]{1,0:T(8,128)(2,1)} %tg.1, bf16[16,128]{1,0:T(8,128)(2,1)} %bitcast.5, bf16[16,2048]{1,0:T(8,128)(2,1)} %hg.1, bf16[128,2048]{1,0:T(8,128)(2,1)} %tu.1, bf16[16,128]{1,0:T(8,128)(2,1)} %bitcast.6, bf16[16,2048]{1,0:T(8,128)(2,1)} %hu.1, ...), custom_call_target="tpu_custom_call" | custom-call | tf_op jit(solution)/shard_map/gather/pallas_call | solution.py:282
  97.9 6.0 %write.1 = (bf16[2048,2048]{1,0:T(8,128)(2,1)}, bf16[2048,2048]{1,0:T(8,128)(2,1)}, f32[1,2048]{1,0:T(1,128)}, f32[1,2048]{1,0:T(1,128)}) custom-call(bf16[2,2048,2048]{2,1,0:T(8,128)(2,1)S(1)} %get-tuple-element.10.new, f32[2,1,2048]{2,1,0:T(1,128)S(1)} %get-tuple-element.11.cmax), custom_call_target="tpu_custom_call" | custom-call | tf_op jit(solution)/shard_map/write/pallas_call | solution.py:311

commit v2 on v1

--- a/solution.py
+++ b/solution.py
@@ -14,16 +14,31 @@
 ROWS = 128
 COLS = 2048
 RANK = 16
-NCB = 8
+NCB = 4
 W = COLS // NCB
-GROUP = 4
-SIDE = 56
+GROUP = 2
+SIDE = 28
+
+
+def rows(src, n=1):
+    return pl.ds(pl.multiple_of(src * ROWS, ROWS), n * ROWS)
+
+
+def columns(cb):
+    return pl.ds(pl.multiple_of(cb * W, W), W)
+
+
+def merged_weights(raw, high, low, gainb, p, src, cb, n):
+    train = raw[p, pl.ds(src, n), cb].reshape(n * ROWS, W).astype(F32)
+    delta = jnp.dot(low[p, rows(src, n), :], high[p, :, columns(cb)], preferred_element_type=F32)
+    scale = gainb[rows(src, n), :]
+    return (train + delta) * jnp.concatenate([scale] * (W // ROWS), axis=1)
 
 
 def gather(
     tg, lg, hg, tu, lu, hu, gn,
-    out, cmax,
-    raw, side, gain, high, low, gainb, part,
+    out, cmax, raw, high, low, gainb, part,
+    side, gain,
     load_sem, side_sem, ring_recv, ring_send, side_send, pair_recv, pair_send, own_recv, own_send,
 ):
     trial, me, cols = lax.axis_index("trial"), lax.axis_index("fsdp"), lax.axis_index("cols")
@@ -119,23 +134,12 @@
 
     lax.fori_loop(0, NCB, send_own, 0)
 
-    def rows(src, n=1):
-        return pl.ds(pl.multiple_of(src * ROWS, ROWS), n * ROWS)
-
     def prepare(src):
         for p in range(2):
             low[p, rows(src), :] = side[src, pl.ds(p * RANK, RANK), :].astype(F32).T.astype(BF16)
         gainb[rows(src), :] = jnp.broadcast_to(gain[src], (ROWS, ROWS)).T
 
-    def merged(p, src, cb, n):
-        train = raw[p, pl.ds(src, n), cb].reshape(n * ROWS, W).astype(F32)
-        delta = jnp.dot(
-            low[p, rows(src, n), :],
-            high[p, :, pl.ds(pl.multiple_of(cb * W, W), W)],
-            preferred_element_type=F32,
-        )
-        scale = gainb[rows(src, n), :]
-        return (train + delta) * jnp.concatenate([scale] * (W // ROWS), axis=1)
+    merged = functools.partial(merged_weights, raw, high, low, gainb)
 
     def note(p, src, cb):
         size = jnp.abs(merged(p, src, cb, 1)).reshape(ROWS // 8, 8, W).max(axis=0)
@@ -163,87 +167,113 @@
 
     lax.fori_loop(0, NCB, note_pair, 0)
 
-    for hops in (1, 2, 3):
+    def pieces(f, hops):
+        for k in range(2 if hops < 4 else 1):
+            for way in range(2):
+                yield way, (way if k == 0 else 1 - way), source(f, way, hops), k
+
+    def at_hop(hops, cb, k):
+        return chunk_at(hops, cb, k) if hops < 4 else 6 * NCB + cb
+
+    def forward(hops, cb, ks=(0, 1)):
+        for way, p, src, k in pieces(me, hops):
+            if k in ks:
+                ring_chunk(way, p, src, cb, at_hop(hops + 1, cb, k)).start()
+
+    def receive(hops, cb, ks=(), relay=True):
+        for way, p, src, k in pieces(me, hops):
+            ring_chunk(way, p, src, cb, at_hop(hops, cb, k)).wait_recv()
+            if k in ks:
+                ring_chunk(way, p, src, cb, at_hop(hops + 1, cb, k)).start()
+            pair_chunk(way, p, src, cb, at_hop(hops, cb, k)).start()
+
+    def note_own_side(hops, cb):
+        for way, p, src, k in pieces(me, hops):
+            note(p, src, cb)
+
+    def note_other_core(hops, cb):
+        for way, p, src, k in pieces(pair, hops):
+            pair_chunk(way, p, src, cb, at_hop(hops, cb, k)).wait_recv()
+            note(p, src, cb)
+
+    def sides(hops):
         for way in range(2):
             src = source(me, way, hops)
             for copy in ring_side(way, src, hops):
                 copy.wait_recv()
-            for copy in ring_side(way, src, hops + 1) + pair_side(way, src, hops):
+            for copy in (ring_side(way, src, hops + 1) if hops < 4 else []) + pair_side(way, src, hops):
                 copy.start()
-            prepare(src)
+            if hops < 4 or way == 1:
+                prepare(src)
         for way in range(2):
             src = source(pair, way, hops)
             for copy in pair_side(way, src, hops):
                 copy.wait_recv()
-            prepare(src)
-
-        def step(cb, _, hops=hops):
-            for k in range(2):
-                for way in range(2):
-                    p, src = (way if k == 0 else 1 - way), source(me, way, hops)
-                    at = chunk_at(hops, cb, k)
-                    ring_chunk(way, p, src, cb, at).wait_recv()
-                    if hops < 3:
-                        ring_chunk(way, p, src, cb, chunk_at(hops + 1, cb, k)).start()
-                    elif k == 0:
-                        ring_chunk(way, p, src, cb, 6 * NCB + cb).start()
-                    pair_chunk(way, p, src, cb, at).start()
-            for k in range(2):
-                for way in range(2):
-                    note(way if k == 0 else 1 - way, source(me, way, hops), cb)
-            for k in range(2):
-                for way in range(2):
-                    p, src = (way if k == 0 else 1 - way), source(pair, way, hops)
-                    pair_chunk(way, p, src, cb, chunk_at(hops, cb, k)).wait_recv()
-                    note(p, src, cb)
-            return 0
-
-        lax.fori_loop(0, NCB, step, 0)
-
-    far, far_pair = source(me, 0, 4), source(pair, 0, 4)
-    for way in range(2):
-        for copy in ring_side(way, far, 4):
-            copy.wait_recv()
-        for copy in pair_side(way, far, 4):
-            copy.start()
-    prepare(far)
-    for way in range(2):
-        for copy in pair_side(way, far_pair, 4):
-            copy.wait_recv()
-    prepare(far_pair)
-
-    def finish(cb):
-        for p in range(2):
-            pair_chunk(p, p, far_pair, cb, 6 * NCB + cb).wait_recv()
-            note(p, far_pair, cb)
+            if hops < 4 or way == 1:
+                prepare(src)
+
+    def scale(cb):
         for p in range(2):
             largest = part[p, cb].max(axis=0, keepdims=True)
-            cmax[p, :, pl.ds(pl.multiple_of(cb * W, W), W)] = largest
+            cmax[p, :, columns(cb)] = largest
             part[p, cb] = jnp.broadcast_to(1.0 / largest, (8, W))
 
-        def scale(i, _):
+        def group(i, _):
             for p in range(2):
                 whole = merged(p, i * GROUP, cb, GROUP) * part[p, cb, :1]
-                out[p, rows(i * GROUP, GROUP), pl.ds(pl.multiple_of(cb * W, W), W)] = whole.astype(BF16)
+                out[p, rows(i * GROUP, GROUP), columns(cb)] = whole.astype(BF16)
             return 0
 
-        lax.fori_loop(0, N // GROUP, scale, 0)
-
-    def last(cb, _):
-        for p in range(2):
-            ring_chunk(p, p, far, cb, 6 * NCB + cb).wait_recv()
-            pair_chunk(p, p, far, cb, 6 * NCB + cb).start()
-        for p in range(2):
-            note(p, far, cb)
-
-        @pl.when(cb > 0)
+        lax.fori_loop(0, N // GROUP, group, 0)
+
+    sides(1)
+
+    def step(cb, _):
+        receive(1, cb, (0, 1))
+        note_own_side(1, cb)
+        note_other_core(1, cb)
+        return 0
+
+    lax.fori_loop(0, NCB, step, 0)
+
+    sides(2)
+
+    def step_2(cb, _):
+        receive(2, cb)
+
+        @pl.when(cb < 2)
         def _():
-            finish(cb - 1)
-
-        return 0
-
-    lax.fori_loop(0, NCB, last, 0)
-    finish(NCB - 1)
+            forward(2, cb)
+
+        note_own_side(2, cb)
+        note_other_core(2, cb)
+        return 0
+
+    lax.fori_loop(0, NCB, step_2, 0)
+    sides(3)
+    sides_due = True
+    for cb in range(NCB):
+        receive(3, cb, (0,))
+        if cb + 2 < NCB:
+            forward(2, cb + 2)
+        note_own_side(3, cb)
+        if cb > 0:
+            if sides_due:
+                sides(4)
+                sides_due = False
+            receive(4, cb - 1)
+            note_own_side(4, cb - 1)
+            note_other_core(3, cb - 1)
+            note_other_core(4, cb - 1)
+            scale(cb - 1)
+    receive(4, NCB - 1)
+    note_own_side(4, NCB - 1)
+    note_other_core(3, NCB - 1)
+    note_other_core(4, NCB - 1)
+    for p in range(2):
+        largest = part[p, NCB - 1].max(axis=0, keepdims=True)
+        cmax[p, :, columns(NCB - 1)] = largest
+        part[p, NCB - 1] = jnp.broadcast_to(1.0 / largest, (8, W))
 
     for way in range(2):
         sent = raw.at[0, pl.ds(0, 7)]
@@ -260,39 +290,63 @@
 
 
 PIECES = 8
-
-
-def write(new, cmax, gate, up, col_gate, col_up, sem):
+DONE = (NCB - 1) * W
+
+
+def write(new, cmax, raw, high, low, gainb, part, gate, up, col_gate, col_up, rest, sem, rest_sem):
     copies = []
-    for p, (dst, col) in enumerate(((gate, col_gate), (up, col_up))):
-        for i in range(PIECES):
-            at = pl.ds(i * (COLS // PIECES), COLS // PIECES)
-            copies.append(pltpu.make_async_copy(new.at[p, at], dst.at[at], sem.at[p, i]))
+    for i in range(PIECES):
+        at = pl.ds(i * (N * ROWS // PIECES), N * ROWS // PIECES)
+        for p, dst in enumerate((gate, up)):
+            copies.append(pltpu.make_async_copy(new.at[p, at], dst.at[at, pl.ds(0, DONE)], sem.at[p, i]))
+    for p, col in enumerate((col_gate, col_up)):
         copies.append(pltpu.make_async_copy(cmax.at[p], col, sem.at[p, PIECES]))
     for copy in copies:
         copy.start()
+
+    def rest_copy(p, i):
+        dst = (gate, up)[p]
+        return pltpu.make_async_copy(
+            rest.at[p, rows(i * GROUP, GROUP)], dst.at[rows(i * GROUP, GROUP), pl.ds(DONE, W)], rest_sem.at[p, i]
+        )
+
+    def group(i, _):
+        for p in range(2):
+            whole = merged_weights(raw, high, low, gainb, p, i * GROUP, NCB - 1, GROUP) * part[p, NCB - 1, :1]
+            rest[p, rows(i * GROUP, GROUP), :] = whole.astype(BF16)
+        for p in range(2):
+            rest_copy(p, i).start()
+        return 0
+
+    lax.fori_loop(0, N // GROUP, group, 0)
     for copy in copies:
         copy.wait()
+    for i in range(N // GROUP):
+        for p in range(2):
+            rest_copy(p, i).wait()
 
 
 def per_device(train_gate, low_gate, high_gate, train_up, low_up, high_up, norm_gain):
-    anywhere = pl.BlockSpec(memory_space=pl.ANY)
+    anywhere = pl.BlockSpec(memory_space=pltpu.HBM)
     vmem = pl.BlockSpec(memory_space=pltpu.VMEM)
     dma = pltpu.SemaphoreType.DMA
-    new, cmax = pl.pallas_call(
+    kept = pl.pallas_call(
         gather,
         name="gather",
-        out_shape=(pltpu.VMEM((2, N * ROWS, COLS), BF16), pltpu.VMEM((2, 1, COLS), F32)),
-        in_specs=[anywhere] * 7,
-        out_specs=(vmem, vmem),
-        scratch_shapes=[
+        out_shape=(
+            pltpu.VMEM((2, N * ROWS, DONE), BF16),
+            pltpu.VMEM((2, 1, COLS), F32),
             pltpu.VMEM((2, N, NCB, ROWS, W), BF16),
-            pltpu.VMEM((N, 2 * RANK, ROWS), BF16),
-            pltpu.VMEM((N, 1, ROWS), F32),
             pltpu.VMEM((2, RANK, COLS), BF16),
             pltpu.VMEM((2, N * ROWS, RANK), BF16),
             pltpu.VMEM((N * ROWS, ROWS), F32),
             pltpu.VMEM((2, NCB, 8, W), F32),
+        ),
+        in_specs=[anywhere] * 7,
+        out_specs=(vmem,) * 7,
+        scratch_shapes=[
+            pltpu.VMEM((N, 2 * RANK, ROWS), BF16),
+            pltpu.VMEM((N, 1, ROWS), F32),
             dma((2, NCB)),
             dma((5,)),
             dma((2, SIDE + 8)),
@@ -304,9 +358,12 @@
             dma((2, 9)),
         ],
         compiler_params=pltpu.CompilerParams(
-            collective_id=0, has_side_effects=True, vmem_limit_bytes=40 * 2**20
+            collective_id=0, has_side_effects=True, vmem_limit_bytes=8 * 2**20
         ),
-    )(train_gate, low_gate.T, high_gate, train_up, low_up.T, high_up, norm_gain.reshape(1, ROWS))
+    )(*(
+        pltpu.with_memory_space_constraint(a, pltpu.HBM)
+        for a in (train_gate, low_gate.T, high_gate, train_up, low_up.T, high_up, norm_gain.reshape(1, ROWS))
+    ))
     hbm = pl.BlockSpec(memory_space=pltpu.HBM)
     gate, up, col_gate, col_up = pl.pallas_call(
         write,
@@ -317,11 +374,11 @@
             jax.ShapeDtypeStruct((1, COLS), F32),
             jax.ShapeDtypeStruct((1, COLS), F32),
         ),
-        in_specs=[vmem, vmem],
+        in_specs=[vmem] * 7,
         out_specs=(hbm,) * 4,
-        scratch_shapes=[dma((2, PIECES + 1))],
-        compiler_params=pltpu.CompilerParams(vmem_limit_bytes=20 * 2**20),
-    )(new, cmax)
+        scratch_shapes=[pltpu.VMEM((2, N * ROWS, W), BF16), dma((2, PIECES + 1)), dma((2, N // GROUP))],
+        compiler_params=pltpu.CompilerParams(vmem_limit_bytes=12 * 2**20),
+    )(*kept)
     return gate, up, col_gate.reshape(COLS), col_up.reshape(COLS)
 
 

time: 104 us -> 100 us (0.962)
  Pallas kernels: 103 us -> 99.5 us
    pallas_call x1, Pallas kernels: 97.3 us -> 93.4 us  [per_device(): pl.pallas_call(gather, name='gather', out_shape=(pltpu.VMEM((2, N * ROWS,...]
where the time goes in v2:
time: 100 us
  Pallas kernels  99.5 us (100%)
    pallas_call x1, Pallas kernels, per_device(): pl.pallas_call(gather, name='gather', out_shape=(pltpu.VMEM((2, N * ROWS,...  93.4 us
    pallas_call x1, Pallas kernels, per_device(): pl.pallas_call(write, name='write', out_shape=(jax.ShapeDtypeStruct((N *...  6.11 us

profile of v2, /device:TPU:1, one launch (start us, length us, event | category | flops | bytes accessed | tf_op | source)
XLA Modules:
  0.0 100.1 jit_solution(472271406410856466)
XLA Ops:
  0.6 93.4 %gather.1 = (bf16[2,2048,1536]{2,1,0:T(8,128)(2,1)S(1)}, f32[2,1,2048]{2,1,0:T(1,128)S(1)}, bf16[2,16,4,128,512]{4,3,2,1,0:T(8,128)(2,1)S(1)}, bf16[2,16,2048]{2...) custom-call(bf16[128,2048]{1,0:T(8,128)(2,1)} %tg.1, ...), custom_call_target="tpu_custom_call" | custom-call | tf_op jit(solution)/shard_map/gather/pallas_call | solution.py:333
  94.0 6.1 %write.1 = (bf16[2048,2048]{1,0:T(8,128)(2,1)}, bf16[2048,2048]{1,0:T(8,128)(2,1)}, f32[1,2048]{1,0:T(1,128)}, f32[1,2048]{1,0:T(1,128)}) custom-call(bf16[2,2048,1536]{2,1,0:T(8,128)(2,1)S(1)} %get-tuple-element.15.new, f32[2,1,2048]{2,1,0:T(1,128)S(1)} %get-tuple-element.16.cmax, bf16[2,16,4,128,512]{4,3,2,1,0:T(8,128)(2,1)S(1)} %get-tuple-element.17.raw, ...), custom_call_target="tpu_custom_call" | custom-call | tf_op jit(solution)/shard_map/write/pallas_call | solution.py:368

commit v3 on v2

--- a/solution.py
+++ b/solution.py
@@ -17,6 +17,8 @@
 NCB = 4
 W = COLS // NCB
 GROUP = 2
+LEFT = 2
+DONE = (NCB - LEFT) * W
 SIDE = 28
 
 
@@ -212,12 +214,13 @@
             if hops < 4 or way == 1:
                 prepare(src)
 
-    def scale(cb):
+    def settle(cb):
         for p in range(2):
             largest = part[p, cb].max(axis=0, keepdims=True)
             cmax[p, :, columns(cb)] = largest
             part[p, cb] = jnp.broadcast_to(1.0 / largest, (8, W))
 
+    def scale(cb):
         def group(i, _):
             for p in range(2):
                 whole = merged(p, i * GROUP, cb, GROUP) * part[p, cb, :1]
@@ -251,29 +254,22 @@
 
     lax.fori_loop(0, NCB, step_2, 0)
     sides(3)
-    sides_due = True
-    for cb in range(NCB):
-        receive(3, cb, (0,))
-        if cb + 2 < NCB:
-            forward(2, cb + 2)
-        note_own_side(3, cb)
-        if cb > 0:
-            if sides_due:
-                sides(4)
-                sides_due = False
-            receive(4, cb - 1)
-            note_own_side(4, cb - 1)
-            note_other_core(3, cb - 1)
-            note_other_core(4, cb - 1)
-            scale(cb - 1)
-    receive(4, NCB - 1)
-    note_own_side(4, NCB - 1)
-    note_other_core(3, NCB - 1)
-    note_other_core(4, NCB - 1)
-    for p in range(2):
-        largest = part[p, NCB - 1].max(axis=0, keepdims=True)
-        cmax[p, :, columns(NCB - 1)] = largest
-        part[p, NCB - 1] = jnp.broadcast_to(1.0 / largest, (8, W))
+    for hops, cb in ((3, 0), (3, 1), (4, 0), (4, 1), (3, 2), (3, 3), (4, 2), (4, 3)):
+        if hops == 4 and cb == 0:
+            sides(4)
+        receive(hops, cb, (0,) if hops == 3 else ())
+        if hops == 3 and cb == 1:
+            forward(2, 2)
+            forward(2, 3)
+        note_own_side(hops, cb)
+        if hops == 4:
+            if cb % 2 == 0:
+                note_other_core(3, cb)
+                note_other_core(3, cb + 1)
+            note_other_core(4, cb)
+            settle(cb)
+            if cb < NCB - LEFT:
+                scale(cb)
 
     for way in range(2):
         sent = raw.at[0, pl.ds(0, 7)]
@@ -290,7 +286,6 @@
 
 
 PIECES = 8
-DONE = (NCB - 1) * W
 
 
 def write(new, cmax, raw, high, low, gainb, part, gate, up, col_gate, col_up, rest, sem, rest_sem):
@@ -304,26 +299,30 @@
     for copy in copies:
         copy.start()
 
-    def rest_copy(p, i):
+    def rest_copy(p, cb, i):
         dst = (gate, up)[p]
         return pltpu.make_async_copy(
-            rest.at[p, rows(i * GROUP, GROUP)], dst.at[rows(i * GROUP, GROUP), pl.ds(DONE, W)], rest_sem.at[p, i]
+            rest.at[p, cb, rows(i * GROUP, GROUP)],
+            dst.at[rows(i * GROUP, GROUP), pl.ds(pl.multiple_of(DONE + cb * W, W), W)],
+            rest_sem.at[p, cb, i],
         )
 
-    def group(i, _):
-        for p in range(2):
-            whole = merged_weights(raw, high, low, gainb, p, i * GROUP, NCB - 1, GROUP) * part[p, NCB - 1, :1]
-            rest[p, rows(i * GROUP, GROUP), :] = whole.astype(BF16)
-        for p in range(2):
-            rest_copy(p, i).start()
-        return 0
-
-    lax.fori_loop(0, N // GROUP, group, 0)
+    def group(j, _):
+        cb, i = j // (N // GROUP), lax.rem(j, N // GROUP)
+        for p in range(2):
+            whole = merged_weights(raw, high, low, gainb, p, i * GROUP, NCB - LEFT + cb, GROUP)
+            rest[p, cb, rows(i * GROUP, GROUP), :] = (whole * part[p, NCB - LEFT + cb, :1]).astype(BF16)
+        for p in range(2):
+            rest_copy(p, cb, i).start()
+        return 0
+
+    lax.fori_loop(0, LEFT * (N // GROUP), group, 0)
     for copy in copies:
         copy.wait()
-    for i in range(N // GROUP):
-        for p in range(2):
-            rest_copy(p, i).wait()
+    for cb in range(LEFT):
+        for i in range(N // GROUP):
+            for p in range(2):
+                rest_copy(p, cb, i).wait()
 
 
 def per_device(train_gate, low_gate, high_gate, train_up, low_up, high_up, norm_gain):
@@ -376,7 +375,7 @@
         ),
         in_specs=[vmem] * 7,
         out_specs=(hbm,) * 4,
-        scratch_shapes=[pltpu.VMEM((2, N * ROWS, W), BF16), dma((2, PIECES + 1)), dma((2, N // GROUP))],
+        scratch_shapes=[pltpu.VMEM((2, LEFT, N * ROWS, W), BF16), dma((2, PIECES + 1)), dma((2, LEFT, N // GROUP))],
         compiler_params=pltpu.CompilerParams(vmem_limit_bytes=12 * 2**20),
     )(*kept)
     return gate, up, col_gate.reshape(COLS), col_up.reshape(COLS)

time: 100 us -> 98.8 us (0.988)
  Pallas kernels: 99.5 us -> 98 us
    pallas_call x1, Pallas kernels: 93.4 us -> 91.8 us  [per_device(): pl.pallas_call(gather, name='gather', out_shape=(pltpu.VMEM((2, N * ROWS,...]
where the time goes in v3:
time: 98.8 us; the launch traced here: 98.7 us
  Pallas kernels  98 us (99%)
    pallas_call x1, Pallas kernels, per_device(): pl.pallas_call(gather, name='gather', out_shape=(pltpu.VMEM((2, N * ROWS,...  91.8 us
    pallas_call x1, Pallas kernels, per_device(): pl.pallas_call(write, name='write', out_shape=(jax.ShapeDtypeStruct((N *...  6.23 us

profile of v3, /device:TPU:1, one launch (start us, length us, event | category | flops | bytes accessed | tf_op | source)
XLA Modules:
  0.0 98.7 jit_solution(11021852660397772260)
XLA Ops:
  0.6 91.8 %gather.1 = (bf16[2,2048,1024]{2,1,0:T(8,128)(2,1)S(1)}, f32[2,1,2048]{2,1,0:T(1,128)S(1)}, bf16[2,16,4,128,512]{4,3,2,1,0:T(8,128)(2,1)S(1)}, bf16[2,16,2048]{2...) custom-call(bf16[128,2048]{1,0:T(8,128)(2,1)} %tg.1, ...), custom_call_target="tpu_custom_call" | custom-call | tf_op jit(solution)/shard_map/gather/pallas_call | solution.py:332
  92.4 6.2 %write.1 = (bf16[2048,2048]{1,0:T(8,128)(2,1)}, bf16[2048,2048]{1,0:T(8,128)(2,1)}, f32[1,2048]{1,0:T(1,128)}, f32[1,2048]{1,0:T(1,128)}) custom-call(bf16[2,2048,1024]{2,1,0:T(8,128)(2,1)S(1)} %get-tuple-element.15.new, f32[2,1,2048]{2,1,0:T(1,128)S(1)} %get-tuple-element.16.cmax, bf16[2,16,4,128,512]{4,3,2,1,0:T(8,128)(2,1)S(1)} %get-tuple-element.17.raw, ...), custom_call_target="tpu_custom_call" | custom-call | tf_op jit(solution)/shard_map/write/pallas_call | solution.py:367

commit v4 on v3

--- a/solution.py
+++ b/solution.py
@@ -19,6 +19,7 @@
 GROUP = 2
 LEFT = 2
 DONE = (NCB - LEFT) * W
+MOVED = 1
 SIDE = 28
 
 
@@ -41,7 +42,7 @@
     tg, lg, hg, tu, lu, hu, gn,
     out, cmax, raw, high, low, gainb, part,
     side, gain,
-    load_sem, side_sem, ring_recv, ring_send, side_send, pair_recv, pair_send, own_recv, own_send,
+    load_sem, side_sem, ring_recv, ring_send, side_send, pair_recv, pair_send, own_recv, own_send, go, moved_send,
 ):
     trial, me, cols = lax.axis_index("trial"), lax.axis_index("fsdp"), lax.axis_index("cols")
     right, left = lax.rem(me + 2, N), lax.rem(me + N - 2, N)
@@ -72,10 +73,24 @@
         for p in range(2):
             own_load(p, cb).start()
 
+    z = me // 2
+    first_right, first_left = z <= 5, (z == 0) | (z == 7)
+    upward_last = (z >= 1) & (z <= 5)
+
     barrier = pltpu.get_barrier_semaphore()
-    for f in (right, left, pair):
-        pl.semaphore_signal(barrier, inc=1, device_id=to(f), device_id_type=MESH)
-    pl.semaphore_wait(barrier, 3)
+    pl.semaphore_signal(barrier, inc=1, device_id=to(pair), device_id_type=MESH)
+    for first, f in ((first_right, right), (first_left, left)):
+
+        @pl.when(first)
+        def _(f=f):
+            pl.semaphore_signal(barrier, inc=1, device_id=to(f), device_id_type=MESH)
+
+    pl.semaphore_wait(barrier, 3 - first_right.astype(jnp.int32) - first_left.astype(jnp.int32))
+    for way, (first, f) in enumerate(((first_right, right), (first_left, left))):
+
+        @pl.when(jnp.logical_not(first))
+        def _(way=way, f=f):
+            pl.semaphore_signal(go.at[1 - way], inc=1, device_id=to(f), device_id_type=MESH)
 
     def remote(ref, send, recv, f):
         return pltpu.make_async_remote_copy(
@@ -117,24 +132,42 @@
 
     for copy in loads:
         copy.wait()
-    for way in range(2):
-        for copy in ring_side(way, me, 1):
+
+    def own_way(way, opening):
+        for copy in ring_side(way, me, 1) + (own_side(me) if opening else []):
             copy.start()
-    for copy in own_side(me):
-        copy.start()
-
-    def send_own(cb, _):
-        for p in range(2):
-            own_load(p, cb).wait()
-        for k in range(2):
-            for way in range(2):
+
+        def block(cb, _):
+            for k in range(2):
                 p = way if k == 0 else 1 - way
+                if opening:
+                    own_load(p, cb).wait()
                 ring_chunk(way, p, me, cb, chunk_at(1, cb, k)).start()
-        for p in range(2):
-            own_chunk(p, me, cb).start()
-        return 0
-
-    lax.fori_loop(0, NCB, send_own, 0)
+                if opening:
+                    own_chunk(p, me, cb).start()
+            return 0
+
+        lax.fori_loop(0, NCB, block, 0)
+
+    @pl.when(upward_last)
+    def _():
+        own_way(1, True)
+        pl.semaphore_wait(go.at[0], 1)
+        own_way(0, False)
+
+    @pl.when(jnp.logical_not(upward_last))
+    def _():
+        @pl.when(z == 0)
+        def _():
+            pl.semaphore_wait(go.at[0], 1)
+
+        own_way(0, True)
+
+        @pl.when(z != 6)
+        def _():
+            pl.semaphore_wait(go.at[1], 1)
+
+        own_way(1, False)
 
     def prepare(src):
         for p in range(2):
@@ -182,11 +215,38 @@
             if k in ks:
                 ring_chunk(way, p, src, cb, at_hop(hops + 1, cb, k)).start()
 
-    def receive(hops, cb, ks=(), relay=True):
+    def moved_chunk(src, cb):
+        return remote(raw.at[0, src, cb], moved_send.at[cb], ring_recv.at[1, SIDE + 8 + cb], left)
+
+    def receive(hops, cb, ks=()):
         for way, p, src, k in pieces(me, hops):
-            ring_chunk(way, p, src, cb, at_hop(hops, cb, k)).wait_recv()
-            if k in ks:
-                ring_chunk(way, p, src, cb, at_hop(hops + 1, cb, k)).start()
+            chunk = ring_chunk(way, p, src, cb, at_hop(hops, cb, k))
+            if hops < 3 or cb < NCB - MOVED or p == 1:
+                chunk.wait_recv()
+                if k in ks:
+                    ring_chunk(way, p, src, cb, at_hop(hops + 1, cb, k)).start()
+            elif hops == 3:
+                chunk.wait_recv()
+                if way == 0:
+
+                    @pl.when(z != 7)
+                    def _(p=p, src=src):
+                        ring_chunk(0, p, src, cb, at_hop(4, cb, 0)).start()
+                else:
+
+                    @pl.when(z == 1)
+                    def _(src=src):
+                        moved_chunk(src, cb).start()
+            else:
+
+                @pl.when(z == 0)
+                def _(src=src):
+                    moved_chunk(src, cb).wait_recv()
+
+                @pl.when(z != 0)
+                def _(chunk=chunk):
+                    chunk.wait_recv()
+
             pair_chunk(way, p, src, cb, at_hop(hops, cb, k)).start()
 
     def note_own_side(hops, cb):
@@ -273,7 +333,23 @@
 
     for way in range(2):
         sent = raw.at[0, pl.ds(0, 7)]
-        pltpu.make_async_copy(sent, sent, ring_send.at[way]).wait()
+        if way == 0:
+            fewer = raw.at[0, pl.ds(0, 9), pl.ds(0, 3)] if MOVED == 1 else raw.at[0, pl.ds(0, 13), pl.ds(0, 2)]
+
+            @pl.when(z == 7)
+            def _(fewer=fewer):
+                pltpu.make_async_copy(fewer, fewer, ring_send.at[0]).wait()
+
+            @pl.when(z != 7)
+            def _(sent=sent):
+                pltpu.make_async_copy(sent, sent, ring_send.at[0]).wait()
+        else:
+            pltpu.make_async_copy(sent, sent, ring_send.at[1]).wait()
+
+            @pl.when(z == 1)
+            def _():
+                for cb in range(NCB - MOVED, NCB):
+                    moved_chunk(source(me, 1, 3), cb).wait_send()
         for hops in (1, 2, 3, 4):
             src = source(me, way, hops - 1)
             for copy in ring_side(way, src, hops):
@@ -348,13 +424,15 @@
             pltpu.VMEM((N, 1, ROWS), F32),
             dma((2, NCB)),
             dma((5,)),
-            dma((2, SIDE + 8)),
+            dma((2, SIDE + 8 + NCB)),
             dma((2,)),
             dma((2, 8)),
             dma((2, SIDE + 8)),
             dma,
             dma((2 * NCB + 2,)),
             dma((2, 9)),
+            pltpu.SemaphoreType.REGULAR((2,)),
+            dma((NCB,)),
         ],
         compiler_params=pltpu.CompilerParams(
             collective_id=0, has_side_effects=True, vmem_limit_bytes=8 * 2**20

time: 98.8 us -> 98 us (level)
  no operation moved by 1% of the time
where the time goes in v4:
time: 98 us; the launch traced here: 97.9 us
  Pallas kernels  97.2 us (99%)
    pallas_call x1, Pallas kernels, per_device(): pl.pallas_call(gather, name='gather', out_shape=(pltpu.VMEM((2, N * ROWS,...  91 us
    pallas_call x1, Pallas kernels, per_device(): pl.pallas_call(write, name='write', out_shape=(jax.ShapeDtypeStruct((N *...  6.23 us

profile of v4, /device:TPU:1, one launch (start us, length us, event | category | flops | bytes accessed | tf_op | source)
XLA Modules:
  0.0 97.9 jit_solution(10922743972025033986)
XLA Ops:
  0.6 91.0 %gather.1 = (bf16[2,2048,1024]{2,1,0:T(8,128)(2,1)S(1)}, f32[2,1,2048]{2,1,0:T(1,128)S(1)}, bf16[2,16,4,128,512]{4,3,2,1,0:T(8,128)(2,1)S(1)}, bf16[2,16,2048]{2...) custom-call(bf16[128,2048]{1,0:T(8,128)(2,1)} %tg.1, ...), custom_call_target="tpu_custom_call" | custom-call | tf_op jit(solution)/shard_map/gather/pallas_call | solution.py:408
  91.6 6.2 %write.1 = (bf16[2048,2048]{1,0:T(8,128)(2,1)}, bf16[2048,2048]{1,0:T(8,128)(2,1)}, f32[1,2048]{1,0:T(1,128)}, f32[1,2048]{1,0:T(1,128)}) custom-call(bf16[2,2048,1024]{2,1,0:T(8,128)(2,1)S(1)} %get-tuple-element.15.new, f32[2,1,2048]{2,1,0:T(1,128)S(1)} %get-tuple-element.16.cmax, bf16[2,16,4,128,512]{4,3,2,1,0:T(8,128)(2,1)S(1)} %get-tuple-element.17.raw, ...), custom_call_target="tpu_custom_call" | custom-call | tf_op jit(solution)/shard_map/write/pallas_call | solution.py:445
